TPU v7x, 512 devices: a whole 4x4x16 slice. The times are simulated.
512 devices in a mesh: cp: 128 (over z, x, core), dp: 4 (over y).
Axes of the slice: x: 4, y: 4, z: 16, core: 2. Of those that a mesh axis runs over, the one named last changes fastest.
Arguments:
- queries: bfloat16 [196608, 1024], P('cp', 'dp'), may hold values from -112 to 112, as said below
- keys: bfloat16 [196608, 128], P('cp'), may hold values from -7 to 7
- values: bfloat16 [196608, 128], P('cp'), may hold values from -6 to 6
- out_grad: bfloat16 [196608, 1024], P('cp', 'dp'), may hold values from -6 to 6
- lengths: int32 [384, 4], P('cp'), may hold values from 1 to 509, as said below
- hop_table: int32 [128, 3], P('cp'), may hold values from 0 to 2, each once within a row
Outputs:
- attn_out: bfloat16 [196608, 1024], P('cp', 'dp')
- query_grad: bfloat16 [196608, 1024], P('cp', 'dp')
- key_grad: bfloat16 [196608, 128], P('cp')
- value_grad: bfloat16 [196608, 128], P('cp')
- row_stats: float32 [8, 196608], P('dp', 'cp')
Inputs may be any that keep to these rules, and one draw needn't show every extreme that they name: Built so that queries and keys stay within this range. `lengths`: each row sums to 512; every slot of the first quarter of the cp loaders begins with a document of at least 384 rows. `hop_table`: each row names every hop once.
All inputs are finite; a program needn't handle non-finite values.
Results may differ from a plain program's by a relative error of at most 0.006.
Values may be sent and summed in bfloat16 or wider, within the bound.
No kernel may reach another device: no remote copies, remote signals or barrier semaphores. Data moves between devices by JAX's collectives and lax.ppermute only.
A program may use at most 128 MiB of HBM per device.

v0:
```python
import jax
import jax.numpy as jnp
from jax import lax
from jax.sharding import PartitionSpec as P


def in_one(arrays, axis):
    ends = [0]
    for a in arrays:
        ends.append(ends[-1] + a.size)
    subtotal = lax.psum(jnp.concatenate([a.ravel() for a in arrays]), axis)
    return tuple((subtotal[b:e].reshape(a.shape) for a, b, e in zip(arrays, ends, ends[1:])))


def passed_along(block, axis, distance):
    devices = range(lax.axis_size(axis))
    route = [((i - distance) % len(devices), i) for i in devices]
    return lax.ppermute(block, axis, route)


def segment_rows(doc_lengths, slot_rows):
    doc_ends = jnp.cumsum(doc_lengths)
    position = jnp.arange(slot_rows, dtype=jnp.int32)
    return jnp.sum((position[:, None] >= doc_ends[None, :]).astype(jnp.int32), axis=1)


def attend(queries, keys, values, out_grad, segment, head_size):
    slot_rows = queries.shape[0]
    head_count = queries.shape[1] // head_size
    score_scale = head_size ** (-0.5)
    block = min(128, slot_rows)
    count = slot_rows // block
    query_heads = queries.reshape(slot_rows, head_count, head_size)
    grad_heads = out_grad.reshape(slot_rows, head_count, head_size)
    position = jnp.arange(slot_rows, dtype=jnp.int32)

    def rows_of(array, index):
        return array[index * block : (index + 1) * block]

    def block_scores(first, second):
        allowed = (rows_of(segment, first)[:, None] == rows_of(segment, second)[None, :]) & (
            rows_of(position, first)[:, None] >= rows_of(position, second)[None, :]
        )
        scores = (
            jnp.einsum(
                "shd,td->hst",
                rows_of(query_heads, first),
                rows_of(keys, second),
                preferred_element_type=jnp.float32,
            )
            * score_scale
        )
        return jnp.where(allowed[None], scores, -jnp.inf)

    def guarded(first, second, compute, empty):
        if first == second:
            return compute()
        needed = segment[(second + 1) * block - 1] >= segment[first * block]
        return lax.cond(needed, compute, lambda: empty)

    out_blocks = []
    qgrad_blocks = []
    stat_blocks = []
    kgrad_blocks = [jnp.zeros((block, head_size), jnp.float32) for second in range(count)]
    vgrad_blocks = [jnp.zeros((block, head_size), jnp.float32) for second in range(count)]
    for first in range(count):
        order = [first] + list(range(first))
        empty_stats = (
            jnp.full((head_count, block), -jnp.inf, jnp.float32),
            jnp.zeros((head_count, block), jnp.float32),
        )
        row_max = None
        row_total = None
        for second in order:

            def max_and_total(second=second):
                scores = block_scores(first, second)
                block_max = jnp.max(scores, axis=2)
                safe_max = jnp.where(jnp.isfinite(block_max), block_max, 0.0)
                return (block_max, jnp.sum(jnp.exp(scores - safe_max[:, :, None]), axis=2))

            block_max, block_total = guarded(first, second, max_and_total, empty_stats)
            if row_max is None:
                row_max, row_total = (block_max, block_total)
            else:
                new_max = jnp.maximum(row_max, block_max)
                safe_block = jnp.where(jnp.isfinite(block_max), block_max, new_max)
                row_total = row_total * jnp.exp(row_max - new_max) + block_total * jnp.exp(
                    safe_block - new_max
                )
                row_max = new_max
        stat_blocks.append(row_max + jnp.log(row_total))

        def probabilities(second):
            return (
                jnp.exp(block_scores(first, second) - row_max[:, :, None]) / row_total[:, :, None]
            )

        output = jnp.zeros((block, head_count, head_size), jnp.float32)
        for second in order:

            def output_part(second=second):
                weights = probabilities(second).astype(jnp.bfloat16)
                return jnp.einsum(
                    "hst,td->shd",
                    weights,
                    rows_of(values, second),
                    preferred_element_type=jnp.float32,
                )

            output = output + guarded(
                first, second, output_part, jnp.zeros((block, head_count, head_size), jnp.float32)
            )
        grad_rows = rows_of(grad_heads, first)
        row_delta = jnp.transpose(jnp.sum(grad_rows.astype(jnp.float32) * output, axis=2))
        query_sum = jnp.zeros((block, head_count, head_size), jnp.float32)
        for second in order:

            def grad_part(second=second):
                softmax = probabilities(second)
                weights = softmax.astype(jnp.bfloat16)
                prob_grad = jnp.einsum(
                    "shd,td->hst",
                    grad_rows,
                    rows_of(values, second),
                    preferred_element_type=jnp.float32,
                )
                score_grad = (softmax * (prob_grad - row_delta[:, :, None])).astype(jnp.bfloat16)
                query_part = jnp.einsum(
                    "hst,td->shd",
                    score_grad,
                    rows_of(keys, second),
                    preferred_element_type=jnp.float32,
                )
                key_part = (
                    jnp.einsum(
                        "hst,shd->td",
                        score_grad,
                        rows_of(query_heads, first),
                        preferred_element_type=jnp.float32,
                    )
                    * score_scale
                )
                value_part = jnp.einsum(
                    "hst,shd->td", weights, grad_rows, preferred_element_type=jnp.float32
                )
                return (query_part, key_part, value_part)

            empty_grads = (
                jnp.zeros((block, head_count, head_size), jnp.float32),
                jnp.zeros((block, head_size), jnp.float32),
                jnp.zeros((block, head_size), jnp.float32),
            )
            query_part, key_part, value_part = guarded(first, second, grad_part, empty_grads)
            query_sum = query_sum + query_part
            kgrad_blocks[second] = kgrad_blocks[second] + key_part
            vgrad_blocks[second] = vgrad_blocks[second] + value_part
        out_blocks.append(output.reshape(block, head_count * head_size).astype(jnp.bfloat16))
        qgrad_blocks.append(
            (query_sum * score_scale).reshape(block, head_count * head_size).astype(jnp.bfloat16)
        )
    return (
        jnp.concatenate(out_blocks, axis=0),
        jnp.concatenate(qgrad_blocks, axis=0),
        jnp.concatenate(kgrad_blocks, axis=0),
        jnp.concatenate(vgrad_blocks, axis=0),
        jnp.concatenate(stat_blocks, axis=1),
    )


def hop_distance(hop_number, cp_count, hop_total):
    return cp_count >> hop_total - hop_number


def pick_slot(hop_row, hop_number, stacked):
    slot_index = jnp.sum(
        jnp.where(hop_row == hop_number, jnp.arange(hop_row.shape[0], dtype=jnp.int32), 0)
    )
    return lax.dynamic_index_in_dim(stacked, slot_index, 0, keepdims=False)


def local(queries, keys, values, out_grad, lengths, hop_table):
    hop_total = lengths.shape[0]
    slot_rows = queries.shape[0] // hop_total
    head_size = keys.shape[1]
    cp_count = lax.axis_size("cp")
    hop_row = hop_table[0]
    segments = jnp.stack(
        [segment_rows(lengths[slot_number], slot_rows) for slot_number in range(hop_total)]
    )
    query_slots = queries.reshape(hop_total, slot_rows, queries.shape[1])
    grad_slots = out_grad.reshape(hop_total, slot_rows, out_grad.shape[1])
    key_slots = keys.reshape(hop_total, slot_rows, head_size)
    value_slots = values.reshape(hop_total, slot_rows, head_size)
    results = [
        attend(
            query_slots[slot_number],
            key_slots[slot_number],
            value_slots[slot_number],
            grad_slots[slot_number],
            segments[slot_number],
            head_size,
        )
        for slot_number in range(hop_total)
    ]
    attn_out = jnp.concatenate([result[0] for result in results], axis=0)
    query_grad = jnp.concatenate([result[1] for result in results], axis=0)
    key_sum, value_sum = in_one(
        (
            jnp.concatenate([result[2] for result in results], axis=0),
            jnp.concatenate([result[3] for result in results], axis=0),
        ),
        "dp",
    )
    stat_slots = jnp.stack([result[4] for result in results])
    gathered = []
    for hop_number in range(hop_total):
        own_stats = pick_slot(hop_row, hop_number, stat_slots)
        if hop_number > 0:
            own_stats = passed_along(own_stats, "cp", hop_distance(hop_number, cp_count, hop_total))
        gathered.append(own_stats)
    row_stats = jnp.concatenate(gathered, axis=1)
    return (
        attn_out,
        query_grad,
        key_sum.astype(jnp.bfloat16),
        value_sum.astype(jnp.bfloat16),
        row_stats,
    )


def solution(mesh):
    return jax.shard_map(
        local,
        mesh=mesh,
        in_specs=(
            P("cp", "dp"),
            P("cp", None),
            P("cp", None),
            P("cp", "dp"),
            P("cp", None),
            P("cp", None),
        ),
        out_specs=(P("cp", "dp"), P("cp", "dp"), P("cp", None), P("cp", None), P("dp", "cp")),
        check_vma=False,
    )
```

profile of v0, /device:TPU:2, one launch (start us, length us, event | category | flops | bytes accessed | tf_op | source)
XLA Modules:
  0.0 431.2 jit_solution(16656267764797365918)
XLA Ops:
  108.9 4.4 %conditional.85 = (f32[2,128]{1,0:T(2,128)}, f32[2,128]{1,0:T(2,128)}, pred[2,128]{1,0:T(4,128)(4,1)}) conditional(s32[]{:T(128)} %bitcast.328, () %tuple.482, (s32[512]{0:T(512)S(1)}, s32[512]{0:T(512)S(1)}, bf16[512,128]{1,0:T(8,128)(2,1)S(1)}, bf16[512,2,128]{0,2,1:T(8,128)(2,1)S(1)}) %tuple.1247), branch_computations={%region_123.124_spmd, %region_124.127_spmd} | conditional | flops 8601600 | bytes 929048 | solution.py:59
  115.4 4.4 %conditional.84 = (f32[2,128]{1,0:T(2,128)}, f32[2,128]{1,0:T(2,128)}, pred[2,128]{1,0:T(4,128)(4,1)}) conditional(s32[]{:T(128)} %bitcast.327, () %tuple.481, (s32[512]{0:T(512)S(1)}, s32[512]{0:T(512)S(1)}, bf16[512,128]{1,0:T(8,128)(2,1)S(1)}, bf16[512,2,128]{0,2,1:T(8,128)(2,1)S(1)}) %tuple.1248), branch_computations={%region_119.120_spmd, %region_120.123_spmd} | conditional | flops 8601600 | bytes 929048 | solution.py:59
  138.3 8.0 %collective-permute-start.1 = (f32[2,512]{1,0:T(2,128)}, f32[2,512]{1,0:T(2,128)}, u32[]{:S(2)}, u32[]{:S(2)}) collective-permute-start(f32[2,512]{1,0:T(2,128)} %get-tuple-element.2909), channel_id=1, source_target_pairs={{256,0},{260,4},{264,8},{268,12},{272,16},{276,20},{280,24},{284,2... | collective-permute-start | bytes 12296 | tf_op jit(solution)/shard_map/ppermute | solution.py:18
  146.2 6.1 %collective-permute-start = (f32[2,512]{1,0:T(2,128)}, f32[2,512]{1,0:T(2,128)}, u32[]{:S(2)}, u32[]{:S(2)}) collective-permute-start(f32[2,512]{1,0:T(2,128)} %get-tuple-element.2910), channel_id=1, source_target_pairs={{384,0},{388,4},{392,8},{396,12},{400,16},{404,20},{408,24},{412,2... | collective-permute-start | bytes 12296 | tf_op jit(solution)/shard_map/ppermute | solution.py:18
  173.0 3.7 conditional.63
  201.2 4.5 %conditional.75 = (f32[128,2,128]{0,2,1:T(8,128)}) conditional(s32[]{:T(128)} %bitcast.294, () %tuple.468, (s32[512]{0:T(512)S(1)}, s32[512]{0:T(512)S(1)}, bf16[512,128]{1,0:T(8,128)(2,1)S(1)}, bf16[512,2,128]{0,2,1:T(8,128)(2,1)S(1)}, f32[2,128]{1,0:T(2,128)S(1)}, /*index=5*/f32[2,128]{1,0:T(2,128)S(1)}, bf16[512,128]{1,0:T(8,128)(2,1)S(1)}) %tuple.1350), branch_computations={%region_86.87_spmd, %region_87.88_spmd} | conditional | flops 16990208 | bytes 1089544 | solution.py:59
  214.6 3.6 conditional.79
  220.8 4.5 %conditional.83 = (f32[128,2,128]{0,2,1:T(8,128)}) conditional(s32[]{:T(128)} %bitcast.320, () %tuple.480, (s32[512]{0:T(512)S(1)}, s32[512]{0:T(512)S(1)}, bf16[512,128]{1,0:T(8,128)(2,1)S(1)}, bf16[512,2,128]{0,2,1:T(8,128)(2,1)S(1)}, f32[2,128]{1,0:T(2,128)}, /*index=5*/f32[2,128]{1,0:T(2,128)}, bf16[512,128]{1,0:T(8,128)(2,1)S(1)}) %tuple.1250), branch_computations={%region_116.117_spmd, %region_117.118_spmd} | conditional | flops 16990208 | bytes 1089544 | solution.py:59
  225.3 4.5 %conditional.82 = (f32[128,2,128]{0,2,1:T(8,128)}) conditional(s32[]{:T(128)} %bitcast.319, () %tuple.478, (s32[512]{0:T(512)S(1)}, s32[512]{0:T(512)S(1)}, bf16[512,128]{1,0:T(8,128)(2,1)S(1)}, bf16[512,2,128]{0,2,1:T(8,128)(2,1)S(1)}, f32[2,128]{1,0:T(2,128)}, /*index=5*/f32[2,128]{1,0:T(2,128)}, bf16[512,128]{1,0:T(8,128)(2,1)S(1)}) %tuple.1251), branch_computations={%region_114.115_spmd, %region_115.116_spmd} | conditional | flops 16990208 | bytes 1089544 | solution.py:59
  238.4 4.5 %conditional.87 = (f32[128,2,128]{0,2,1:T(8,128)}) conditional(s32[]{:T(128)} %bitcast.327, () %tuple.484, (s32[512]{0:T(512)S(1)}, s32[512]{0:T(512)S(1)}, bf16[512,128]{1,0:T(8,128)(2,1)S(1)}, bf16[512,2,128]{0,2,1:T(8,128)(2,1)S(1)}, f32[2,128]{1,0:T(2,128)}, /*index=5*/f32[2,128]{1,0:T(2,128)}, bf16[512,128]{1,0:T(8,128)(2,1)S(1)}) %tuple.1254), branch_computations={%region_132.133_spmd, %region_133.134_spmd} | conditional | flops 16990208 | bytes 1089544 | solution.py:59
  249.6 6.2 %conditional.90 = (f32[128,128]{1,0:T(8,128)}, f32[128,128]{1,0:T(8,128)}, f32[128,2,128]{0,2,1:T(8,128)}) conditional(s32[]{:T(128)} %bitcast.245, () %tuple.488, (s32[512]{0:T(512)S(1)}, s32[512]{0:T(512)S(1)}, bf16[512,128]{1,0:T(8,128)(2,1)S(1)}, bf16[512,2,128]{0,2,1:T(8,128)(2,1)S(1)}, f32[2,128]{1,0:T(2,128)}, ...), branch_computations={%region_140.141_spmd, %region_141.142_spmd} | conditional | flops 42270720 | bytes 2040856 | solution.py:59
  260.0 6.9 %conditional.92 = (f32[128,128]{1,0:T(8,128)}, f32[128,128]{1,0:T(8,128)}, f32[128,2,128]{0,2,1:T(8,128)}) conditional(s32[]{:T(128)} %bitcast.254, () %tuple.492, (s32[512]{0:T(512)S(1)}, s32[512]{0:T(512)}, bf16[512,128]{1,0:T(8,128)(2,1)S(1)}, bf16[512,2,128]{0,2,1:T(8,128)(2,1)S(1)}, f32[2,128]{1,0:T(2,128)}, ...), branch_computations={%region_145.146_spmd, %region_146.147_spmd} | conditional | flops 42270720 | bytes 2040856 | solution.py:59
  266.8 6.9 %conditional.91 = (f32[128,128]{1,0:T(8,128)}, f32[128,128]{1,0:T(8,128)}, f32[128,2,128]{0,2,1:T(8,128)}) conditional(s32[]{:T(128)} %bitcast.253, () %tuple.490, (s32[512]{0:T(512)S(1)}, s32[512]{0:T(512)}, bf16[512,128]{1,0:T(8,128)(2,1)S(1)}, bf16[512,2,128]{0,2,1:T(8,128)(2,1)S(1)}, f32[2,128]{1,0:T(2,128)}, ...), branch_computations={%region_143.144_spmd, %region_144.145_spmd} | conditional | flops 42270720 | bytes 2040856 | solution.py:59
  278.1 7.8 %conditional.95 = (f32[128,128]{1,0:T(8,128)}, f32[128,128]{1,0:T(8,128)}, f32[128,2,128]{0,2,1:T(8,128)S(1)}) conditional(s32[]{:T(128)} %bitcast.263, () %tuple.496, (s32[512]{0:T(512)S(1)}, s32[512]{0:T(512)}, bf16[512,128]{1,0:T(8,128)(2,1)S(1)}, bf16[512,2,128]{0,2,1:T(8,128)(2,1)S(1)}, f32[2,128]{1,0:T(2,128)}, ...), branch_computations={%region_152.153_spmd, %region_153.154_spmd} | conditional | flops 42270720 | bytes 2040856 | solution.py:59
  285.9 8.5 %conditional.94 = (f32[128,128]{1,0:T(8,128)}, f32[128,128]{1,0:T(8,128)}, f32[128,2,128]{0,2,1:T(8,128)}) conditional(s32[]{:T(128)} %bitcast.262, () %tuple.495, (s32[512]{0:T(512)S(1)}, s32[512]{0:T(512)}, bf16[512,128]{1,0:T(8,128)(2,1)S(1)}, bf16[512,2,128]{0,2,1:T(8,128)(2,1)S(1)}, f32[2,128]{1,0:T(2,128)}, ...), branch_computations={%region_150.151_spmd, %region_151.152_spmd} | conditional | flops 42270720 | bytes 2040856 | solution.py:59
  294.4 6.9 %conditional.93 = (f32[128,128]{1,0:T(8,128)}, f32[128,128]{1,0:T(8,128)}, f32[128,2,128]{0,2,1:T(8,128)S(1)}) conditional(s32[]{:T(128)} %bitcast.261, () %tuple.493, (s32[512]{0:T(512)S(1)}, s32[512]{0:T(512)}, bf16[512,128]{1,0:T(8,128)(2,1)S(1)}, bf16[512,2,128]{0,2,1:T(8,128)(2,1)S(1)}, f32[2,128]{1,0:T(2,128)}, ...), branch_computations={%region_148.149_spmd, %region_149.150_spmd} | conditional | flops 42270720 | bytes 2040856 | solution.py:59
  306.3 5.5 %conditional.96 = (f32[128,128]{1,0:T(8,128)}, f32[128,128]{1,0:T(8,128)}, f32[128,2,128]{0,2,1:T(8,128)S(1)}) conditional(s32[]{:T(128)} %bitcast.278, () %tuple.497, (s32[512]{0:T(512)S(1)}, s32[512]{0:T(512)S(1)}, bf16[512,128]{1,0:T(8,128)(2,1)S(1)}, bf16[512,2,128]{0,2,1:T(8,128)(2,1)S(1)}, f32[2,128]{1,0:T(2,128)S(1)}, ...), branch_computations={%region_156.157_spmd, %region_157.158_spmd} | conditional | flops 42270720 | bytes 3097708 | solution.py:59
  314.9 4.8 %conditional.98 = (f32[128,128]{1,0:T(8,128)S(1)}, f32[128,128]{1,0:T(8,128)}, f32[128,2,128]{0,2,1:T(8,128)S(1)}) conditional(s32[]{:T(128)} %bitcast.287, () %tuple.501, (s32[512]{0:T(512)S(1)}, s32[512]{0:T(512)}, bf16[512,128]{1,0:T(8,128)(2,1)S(1)}, bf16[512,2,128]{0,2,1:T(8,128)(2,1)S(1)}, f32[2,128]{1,0:T(2,128)}, ...), branch_computations={%region_161.162_spmd, %region_162.163_spmd} | conditional | flops 42270720 | bytes 3089460 | solution.py:59
  319.7 6.3 %conditional.97 = (f32[128,128]{1,0:T(8,128)S(1)}, f32[128,128]{1,0:T(8,128)}, f32[128,2,128]{0,2,1:T(8,128)}) conditional(s32[]{:T(128)} %bitcast.286, () %tuple.499, (s32[512]{0:T(512)S(1)}, s32[512]{0:T(512)}, bf16[512,128]{1,0:T(8,128)(2,1)S(1)}, bf16[512,2,128]{0,2,1:T(8,128)(2,1)S(1)}, f32[2,128]{1,0:T(2,128)}, ...), branch_computations={%region_159.160_spmd, %region_160.161_spmd} | conditional | flops 42270720 | bytes 2040856 | solution.py:59
  329.5 3.5 conditional.101
  333.7 4.1 conditional.100
  338.4 4.3 conditional.99
  366.7 4.9 %conditional.105 = (f32[128,128]{1,0:T(8,128)}, f32[128,128]{1,0:T(8,128)}, f32[128,2,128]{0,2,1:T(8,128)S(1)}) conditional(s32[]{:T(128)} %bitcast.327, () %tuple.511, (s32[512]{0:T(512)S(1)}, s32[512]{0:T(512)S(1)}, bf16[512,128]{1,0:T(8,128)(2,1)S(1)}, bf16[512,2,128]{0,2,1:T(8,128)(2,1)S(1)}, f32[2,128]{1,0:T(2,128)}, ...), branch_computations={%region_180.181_spmd, %region_181.182_spmd} | conditional | flops 42270720 | bytes 2040856 | solution.py:59
  391.0 36.8 %all-reduce.1 = bf16[393216]{0:T(1024)(128)(2,1)S(1)} all-reduce(f32[393216]{0:T(1024)S(1)} %pad_maximum_fusion), channel_id=1, replica_groups=mesh['cp'=128,'dp'=4] {'dp'}, use_global_device_ids=true, to_apply=%region_186.187 | all-reduce | flops 393216 | bytes 2359296 | tf_op jit(solution)/shard_map/psum | solution.py:11
  (1049 shorter events, 422.1 us)
Async XLA Ops:
  3.0 20.3 %copy-start.201 = (s32[1,3]{1,0:T(1,128)S(1)}, s32[1,3]{1,0:T(1,128)}, u32[]{:S(2)}) copy-start(s32[1,3]{1,0:T(1,128)} %param.119) | copy-start | bytes 40
  3.0 25.9 %copy-start = (bf16[1536,128]{1,0:T(8,128)(2,1)S(1)}, bf16[1536,128]{1,0:T(8,128)(2,1)}, u32[]{:S(2)}) copy-start(bf16[1536,128]{1,0:T(8,128)(2,1)} %param.115) | copy-start | bytes 1179652
  3.0 28.4 %copy-start.42 = (bf16[1536,128]{1,0:T(8,128)(2,1)S(1)}, bf16[1536,128]{1,0:T(8,128)(2,1)}, u32[]{:S(2)}) copy-start(bf16[1536,128]{1,0:T(8,128)(2,1)} %param.116) | copy-start | bytes 1179652
  5.0 27.5 %copy-start.60 = (bf16[128,256]{1,0:T(8,128)(2,1)S(1)}, bf16[128,256]{1,0:T(8,128)(2,1)}, u32[]{:S(2)}) copy-start(bf16[128,256]{1,0:T(8,128)(2,1)} %get-tuple-element.2872) | copy-start | bytes 196612
  29.6 22.9 %copy-start.135 = (f32[2,128]{1,0:T(2,128)}, f32[2,128]{1,0:T(2,128)S(1)}, u32[]{:S(2)}) copy-start(f32[2,128]{1,0:T(2,128)S(1)} %get-tuple-element.2965) | copy-start | bytes 3076
  31.4 9.3 %copy-start.56 = (bf16[128,256]{1,0:T(8,128)(2,1)S(1)}, bf16[128,256]{1,0:T(8,128)(2,1)}, u32[]{:S(2)}) copy-start(bf16[128,256]{1,0:T(8,128)(2,1)} %get-tuple-element.2866) | copy-start | bytes 196612
  31.9 42.6 %copy-start.6 = (f32[2,128,128]{1,2,0:T(8,128)}, f32[2,128,128]{1,2,0:T(8,128)S(1)}, u32[]{:S(2)}) copy-start(f32[2,128,128]{1,2,0:T(8,128)S(1)} %get-tuple-element.2969) | copy-start | bytes 393220
  32.5 12.9 %copy-start.55 = (bf16[128,256]{1,0:T(8,128)(2,1)S(1)}, bf16[128,256]{1,0:T(8,128)(2,1)}, u32[]{:S(2)}) copy-start(bf16[128,256]{1,0:T(8,128)(2,1)} %get-tuple-element.2864) | copy-start | bytes 196612
  36.2 15.6 %copy-start.3 = (f32[2,128,128]{1,2,0:T(8,128)S(1)}, f32[2,128,128]{1,2,0:T(8,128)}, u32[]{:S(2)}) copy-start(f32[2,128,128]{1,2,0:T(8,128)} %get-tuple-element.2966) | copy-start | bytes 393220
  38.4 11.5 %copy-start.9 = (f32[2,128,128]{1,2,0:T(8,128)S(1)}, f32[2,128,128]{1,2,0:T(8,128)}, u32[]{:S(2)}) copy-start(f32[2,128,128]{1,2,0:T(8,128)} %get-tuple-element.2978) | copy-start | bytes 393220
  38.7 40.7 %copy-start.12 = (f32[2,128,128]{1,2,0:T(8,128)}, f32[2,128,128]{1,2,0:T(8,128)S(1)}, u32[]{:S(2)}) copy-start(f32[2,128,128]{1,2,0:T(8,128)S(1)} %get-tuple-element.2981) | copy-start | bytes 393220
  44.7 52.4 %copy-start.17 = (f32[2,128,128]{1,2,0:T(8,128)}, f32[2,128,128]{1,2,0:T(8,128)S(1)}, u32[]{:S(2)}) copy-start(f32[2,128,128]{1,2,0:T(8,128)S(1)} %get-tuple-element.2993) | copy-start | bytes 393220
  62.5 12.1 %copy-start.20 = (f32[2,128,128]{1,2,0:T(8,128)}, f32[2,128,128]{1,2,0:T(8,128)S(1)}, u32[]{:S(2)}) copy-start(f32[2,128,128]{1,2,0:T(8,128)S(1)} %get-tuple-element.2972) | copy-start | bytes 393220
  108.9 43.4 %copy-start.2 = (bf16[1536,256]{1,0:T(8,128)(2,1)S(1)}, bf16[1536,256]{1,0:T(8,128)(2,1)}, u32[]{:S(2)}) copy-start(bf16[1536,256]{1,0:T(8,128)(2,1)} %param.117) | copy-start | bytes 2359300
  138.3 291.6 %collective-permute-start.1 = (f32[2,512]{1,0:T(2,128)}, f32[2,512]{1,0:T(2,128)}, u32[]{:S(2)}, u32[]{:S(2)}) collective-permute-start(f32[2,512]{1,0:T(2,128)} %get-tuple-element.2909), channel_id=1, source_target_pairs={{256,0},{260,4},{264,8},{268,12},{272,16},{276,20},{280,24},{284,2... | collective-permute-start | bytes 12296 | tf_op jit(solution)/shard_map/ppermute | solution.py:18
  146.2 283.7 %collective-permute-start = (f32[2,512]{1,0:T(2,128)}, f32[2,512]{1,0:T(2,128)}, u32[]{:S(2)}, u32[]{:S(2)}) collective-permute-start(f32[2,512]{1,0:T(2,128)} %get-tuple-element.2910), channel_id=1, source_target_pairs={{384,0},{388,4},{392,8},{396,12},{400,16},{404,20},{408,24},{412,2... | collective-permute-start | bytes 12296 | tf_op jit(solution)/shard_map/ppermute | solution.py:18
  208.1 10.1 %copy-start.18 = (f32[2,128,128]{1,2,0:T(8,128)S(1)}, f32[2,128,128]{1,2,0:T(8,128)}, u32[]{:S(2)}) copy-start(f32[2,128,128]{1,2,0:T(8,128)} %copy-done.17) | copy-start | bytes 393220
  209.9 10.8 %copy-start.49 = (bf16[128,256]{1,0:T(8,128)(2,1)S(1)}, bf16[128,256]{1,0:T(8,128)(2,1)}, u32[]{:S(2)}) copy-start(bf16[128,256]{1,0:T(8,128)(2,1)} %get-tuple-element.2862) | copy-start | bytes 196612
  220.8 9.0 %copy-start.35 = (f32[2,128,128]{1,2,0:T(8,128)S(1)}, f32[2,128,128]{1,2,0:T(8,128)}, u32[]{:S(2)}) copy-start(f32[2,128,128]{1,2,0:T(8,128)} %copy-done.34) | copy-start | bytes 393220
  390.9 38.0 %copy-start.66 = (bf16[128,256]{1,0:T(8,128)(2,1)S(1)}, bf16[128,256]{1,0:T(8,128)(2,1)}, u32[]{:S(2)}) copy-start(bf16[128,256]{1,0:T(8,128)(2,1)} %copy.648) | copy-start | bytes 196612
  390.9 38.0 %copy-start.146 = (bf16[1536,256]{1,0:T(8,128)(2,1)S(1)}, bf16[1536,256]{1,0:T(8,128)(2,1)}, u32[]{:S(2)}) copy-start(bf16[1536,256]{1,0:T(8,128)(2,1)} %constant_dynamic-update-slice_fusion.11) | copy-start | bytes 2359300
  390.9 38.0 %copy-start.67 = (bf16[128,256]{1,0:T(8,128)(2,1)S(1)}, bf16[128,256]{1,0:T(8,128)(2,1)}, u32[]{:S(2)}) copy-start(bf16[128,256]{1,0:T(8,128)(2,1)} %copy.649) | copy-start | bytes 196612
  390.9 38.0 %copy-start.68 = (bf16[128,256]{1,0:T(8,128)(2,1)S(1)}, bf16[128,256]{1,0:T(8,128)(2,1)}, u32[]{:S(2)}) copy-start(bf16[128,256]{1,0:T(8,128)(2,1)} %copy.650) | copy-start | bytes 196612
  391.0 38.0 %copy-start.69 = (bf16[128,256]{1,0:T(8,128)(2,1)S(1)}, bf16[128,256]{1,0:T(8,128)(2,1)}, u32[]{:S(2)}) copy-start(bf16[128,256]{1,0:T(8,128)(2,1)} %copy.651) | copy-start | bytes 196612
  (185 other events, 764.8 us)
where the time goes:
time: 438 us; the launch traced here: 431 us
  matrix products  171 us (39%)
  local copies, waits for them, and re-layouts  103 us (24%)
  other arithmetic  72.8 us (17%)
  blocking collectives  36.8 us (8%)
  between operations  32.5 us (7%)
  starting transfers between devices  14 us (3%)
    dot_general x30, matrix products, output_part(): jnp.einsum('hst,td->shd', weights, rows_of(values, second), preferred_ele...  43 us
    dot_general x48, matrix products, block_scores(): jnp.einsum('shd,td->hst', rows_of(query_heads, first), rows_of(keys, seco...  39.7 us
    psum x1, blocking collectives, in_one(): subtotal = lax.psum(jnp.concatenate([a.ravel() for a in arrays]), axis)  36.8 us
    dot_general x30, matrix products, grad_part(): jnp.einsum('shd,td->hst', grad_rows, rows_of(values, second), preferred_e...  28.4 us
    dot_general x30, matrix products, grad_part(): jnp.einsum('hst,shd->td', score_grad, rows_of(query_heads, first), prefer...  27.1 us
    another operation x55, local copies, waits for them, and re-layouts  26 us
    select_n x27, other arithmetic, max_and_total(): safe_max = jnp.where(jnp.isfinite(block_max), block_max, 0.0)  24.4 us
    cond x36, local copies, waits for them, and re-layouts, guarded(): return lax.cond(needed, compute, lambda: empty)  22.2 us
  transfers between devices with their start and end apart: 2, of which 0 were waited for; matrix products, arithmetic and copies ran while one was open for 53% of the time, Pallas kernels for 0%

commit v1 on v0

v1 whole, which is shorter than its diff:
```python
import functools
import math

import jax
import jax.numpy as jnp
from jax import lax
from jax.experimental import pallas as pl
from jax.experimental.pallas import tpu as pltpu
from jax.sharding import PartitionSpec as P

BLOCK = 128


def slot_body(
    order,
    lengths,
    queries,
    keys,
    values,
    out_grad,
    attn_out,
    query_grad,
    partial,
    stats,
    key_sum,
    value_sum,
    *,
    heads,
    scale,
):
    rows, head_size = keys.shape
    blocks = rows // BLOCK
    wide = heads * BLOCK
    slot = order[pl.program_id(0)]
    first_end = lengths[slot, 0]
    second_end = first_end + lengths[slot, 1]
    third_end = second_end + lengths[slot, 2]
    value_cols = jnp.transpose(values[...])
    key_cols = jnp.transpose(keys[...])
    to_exp2 = scale * math.log2(math.e)
    nt = (((1,), (1,)), ((), ()))
    nn = (((1,), (0,)), ((), ()))
    lane = lax.broadcasted_iota(jnp.int32, (1, wide), 1) % BLOCK

    def stacked(ref, begin):
        return jnp.concatenate(
            [
                ref[begin : begin + BLOCK, h * head_size : (h + 1) * head_size]
                for h in range(heads)
            ],
            axis=0,
        )

    for block in reversed(range(blocks)):
        begin = block * BLOCK
        span = begin + BLOCK
        query_rows = stacked(queries, begin)
        grad_rows = stacked(out_grad, begin)
        row = lane + begin
        start = jnp.where(
            row >= third_end,
            third_end,
            jnp.where(row >= second_end, second_end, jnp.where(row >= first_end, first_end, 0)),
        )
        col = lax.broadcasted_iota(jnp.int32, (span, wide), 0)
        allowed = (col >= start) & (col <= row)
        scores = lax.dot_general(
            keys[0:span, :], query_rows, nt, preferred_element_type=jnp.float32
        )
        scores = jnp.where(allowed, scores, -jnp.inf)
        row_max = jnp.max(scores, axis=0, keepdims=True)
        exp_scores = jnp.exp2((scores - row_max) * to_exp2)
        row_total = jnp.sum(exp_scores, axis=0, keepdims=True)
        softmax = exp_scores * (1.0 / row_total)
        log_total = row_max * scale + jnp.log(row_total)
        for h in range(heads):
            stats[0, h : h + 1, begin:span] = log_total[:, h * BLOCK : (h + 1) * BLOCK]
        weights = softmax.astype(jnp.bfloat16)
        prob_grad = lax.dot_general(
            values[0:span, :], grad_rows, nt, preferred_element_type=jnp.float32
        )
        delta = jnp.sum(weights.astype(jnp.float32) * prob_grad, axis=0, keepdims=True)
        score_grad = (softmax * (prob_grad - delta)).astype(jnp.bfloat16)
        output = lax.dot_general(
            value_cols[:, 0:span], weights, nn, preferred_element_type=jnp.float32
        )
        query_sum = lax.dot_general(
            key_cols[:, 0:span], score_grad, nn, preferred_element_type=jnp.float32
        )
        output = jnp.transpose(output.astype(jnp.bfloat16))
        query_sum = jnp.transpose((query_sum * scale).astype(jnp.bfloat16))
        for h in range(heads):
            at = slice(h * BLOCK, (h + 1) * BLOCK)
            attn_out[begin:span, h * head_size : (h + 1) * head_size] = output[at]
            query_grad[begin:span, h * head_size : (h + 1) * head_size] = query_sum[at]
        value_part = lax.dot_general(weights, grad_rows, nn, preferred_element_type=jnp.float32)
        key_part = lax.dot_general(score_grad, query_rows, nn, preferred_element_type=jnp.float32)
        if block == blocks - 1:
            value_sum[...] = value_part
            key_sum[...] = key_part
        else:
            value_sum[0:span, :] += value_part
            key_sum[0:span, :] += key_part
    partial[0] = (key_sum[...] * scale).astype(partial.dtype)
    partial[1] = value_sum[...].astype(partial.dtype)


def attend(order, lengths, queries, keys, values, out_grad):
    slots = lengths.shape[0]
    rows = keys.shape[0] // slots
    head_size = keys.shape[1]
    width = queries.shape[1]
    heads = width // head_size
    wide_spec = pl.BlockSpec((rows, width), lambda i, order, lengths: (order[i], 0))
    narrow_spec = pl.BlockSpec((rows, head_size), lambda i, order, lengths: (order[i], 0))
    return pl.pallas_call(
        functools.partial(slot_body, heads=heads, scale=head_size**-0.5),
        grid_spec=pltpu.PrefetchScalarGridSpec(
            num_scalar_prefetch=2,
            grid=(slots,),
            in_specs=[wide_spec, narrow_spec, narrow_spec, wide_spec],
            out_specs=[
                wide_spec,
                wide_spec,
                pl.BlockSpec((2, rows, head_size), lambda i, order, lengths: (0, order[i], 0)),
                pl.BlockSpec((1, heads, rows), lambda i, order, lengths: (i, 0, 0)),
            ],
            scratch_shapes=[
                pltpu.VMEM((rows, head_size), jnp.float32),
                pltpu.VMEM((rows, head_size), jnp.float32),
            ],
        ),
        out_shape=[
            jax.ShapeDtypeStruct(queries.shape, jnp.bfloat16),
            jax.ShapeDtypeStruct(queries.shape, jnp.bfloat16),
            jax.ShapeDtypeStruct((2,) + keys.shape, jnp.bfloat16),
            jax.ShapeDtypeStruct((slots, heads, rows), jnp.float32),
        ],
        name="attend",
    )(order, lengths, queries, keys, values, out_grad)


def passed_along(block, axis, distance):
    devices = range(lax.axis_size(axis))
    route = [((i - distance) % len(devices), i) for i in devices]
    return lax.ppermute(block, axis, route)


def local(queries, keys, values, out_grad, lengths, hop_table):
    hops = lengths.shape[0]
    cp_count = lax.axis_size("cp")
    dp_count = lax.axis_size("dp")
    hop = jnp.arange(hops, dtype=jnp.int32)
    order = jnp.sum(jnp.where(hop_table[0][None, :] == hop[:, None], hop[None, :], 0), axis=1)
    attn_out, query_grad, partial, stats = attend(
        order.astype(jnp.int32), lengths, queries, keys, values, out_grad
    )
    gathered = [stats[0]] + [
        passed_along(stats[b], "cp", cp_count >> (hops - b)) for b in range(1, hops)
    ]
    row_stats = jnp.concatenate(gathered, axis=1)
    pieces = partial.reshape(dp_count, -1, partial.shape[-1])
    pieces = lax.all_to_all(pieces, "dp", 0, 0)
    first, second, third, fourth = (pieces[i].astype(jnp.float32) for i in range(dp_count))
    piece = ((first + second) + (third + fourth)).astype(jnp.bfloat16)
    whole = lax.all_gather(piece, "dp", axis=0, tiled=True).reshape(partial.shape)
    return (attn_out, query_grad, whole[0], whole[1], row_stats)


def solution(mesh):
    return jax.shard_map(
        local,
        mesh=mesh,
        in_specs=(
            P("cp", "dp"),
            P("cp", None),
            P("cp", None),
            P("cp", "dp"),
            P("cp", None),
            P("cp", None),
        ),
        out_specs=(P("cp", "dp"), P("cp", "dp"), P("cp", None), P("cp", None), P("dp", "cp")),
        check_vma=False,
    )
```

time: 438 us -> 58.2 us (0.13)
  the two profiles are of different devices: /device:TPU:2 before, /device:TPU:4 now
where the time goes in v1:
time: 58.2 us; the launch traced here: 57.8 us
  starting transfers between devices  24.5 us (42%)
  blocking collectives  15.1 us (26%)
  Pallas kernels  9.57 us (16%)
  waiting for transfers between devices  5.12 us (9%)
  local copies, waits for them, and re-layouts  1.58 us (3%)
  other arithmetic  1.34 us (2%)
  between operations  0.67 us (1%)
    ppermute x2, starting transfers between devices, passed_along(): return lax.ppermute(block, axis, route)  20 us
    all_gather x1, blocking collectives, local(): lax.all_gather(piece, 'dp', axis=0, tiled=True).reshape(partial.shape)  15.1 us
    pallas_call x1, Pallas kernels, attend(): pl.pallas_call(functools.partial(slot_body, heads=heads, scale=head_size...  9.57 us
    ppermute x2, waiting for transfers between devices, passed_along(): return lax.ppermute(block, axis, route)  5.12 us
    all_to_all x1, starting transfers between devices, local(): pieces = lax.all_to_all(pieces, 'dp', 0, 0)  4.47 us
  transfers between devices with their start and end apart: 3, of which 1 were waited for; matrix products, arithmetic and copies ran while one was open for 1% of the time, Pallas kernels for 0%

profile of v1, /device:TPU:4, one launch (start us, length us, event | category | flops | bytes accessed | tf_op | source)
XLA Modules:
  0.0 57.8 jit_solution(5311725040836288203)
XLA Ops:
  0.6 0.0 copy-start.1
  0.6 0.6 %copy-done.1 = s32[1,3]{1,0:T(1,128)S(1)} copy-done((s32[1,3]{1,0:T(1,128)S(1)}, s32[1,3]{1,0:T(1,128)}, u32[]{:S(2)}) %copy-start.1) | copy-done | bytes 36
  1.3 0.6 %select_reduce_fusion.order = s32[3]{0:T(128)} fusion(s32[3]{0:T(128)S(1)} %bitcast.13), kind=kLoop, calls=%fused_computation.7 | loop fusion | flops 24 | bytes 24 | tf_op jit(solution)/shard_map/reduce_sum | solution.py:154
  1.9 9.6 %attend.1 = (bf16[1536,256]{1,0:T(8,128)(2,1)}, bf16[1536,256]{1,0:T(8,128)(2,1)}, bf16[2,1536,128]{2,1,0:T(8,128)(2,1)}, f32[3,2,512]{2,1,0:T(2,128)}) custom-call(s32[3]{0:T(128)} %select_reduce_fusion.order, s32[3,4]{1,0:T(4,128)} %lengths.1, bf16[1536,256]{1,0:T(8,128)(2,1)} %queries.1, bf16[1536,128]{1,0:T(8,128)(2,1)} %keys.1, ...), custom_call_target="tpu_custom_call" | custom-call | tf_op jit(solution)/shard_map/attend/pallas_call | solution.py:116
  11.5 0.0 copy-start
  11.5 4.5 %all-to-all-start = ((bf16[4,768,128]{2,1,0:T(8,128)(2,1)}), bf16[4,768,128]{2,1,0:T(8,128)(2,1)S(1)}, u32[]{:S(2)}, u32[]{:S(2)}) async-start(bf16[4,768,128]{2,1,0:T(8,128)(2,1)} %bitcast.12), calls=%async_computation | async-start | bytes 1572864 | tf_op jit(solution)/shard_map/all_to_all | solution.py:163
  16.0 0.0 copy-done
  16.0 15.7 %collective-permute-start.1 = (f32[2,512]{1,0:T(2,128)S(1)}, f32[2,512]{1,0:T(2,128)S(1)}, u32[]{:S(2)}, u32[]{:S(2)}) collective-permute-start(f32[2,512]{1,0:T(2,128)S(1)} %get-tuple-element.16), channel_id=1, source_target_pairs={{256,0},{260,4},{264,8},{268,12},{272,16},{276,20},{280,24},{284,2... | collective-permute-start | bytes 12296 | tf_op jit(solution)/shard_map/ppermute | solution.py:146
  31.7 4.3 %collective-permute-start = (f32[2,512]{1,0:T(2,128)S(1)}, f32[2,512]{1,0:T(2,128)S(1)}, u32[]{:S(2)}, u32[]{:S(2)}) collective-permute-start(f32[2,512]{1,0:T(2,128)S(1)} %get-tuple-element.17), channel_id=1, source_target_pairs={{384,0},{388,4},{392,8},{396,12},{400,16},{404,20},{408,24},{412,2... | collective-permute-start | bytes 12296 | tf_op jit(solution)/shard_map/ppermute | solution.py:146
  36.0 0.0 collective-permute-done.1
  36.0 5.1 %collective-permute-done = f32[2,512]{1,0:T(2,128)S(1)} collective-permute-done((f32[2,512]{1,0:T(2,128)S(1)}, f32[2,512]{1,0:T(2,128)S(1)}, u32[]{:S(2)}, u32[]{:S(2)}) %collective-permute-start) | collective-permute-done | bytes 4128 | tf_op jit(solution)/shard_map/ppermute | solution.py:146
  41.1 0.6 %pad_maximum_fusion = f32[2,1536]{1,0:T(2,128)} fusion(f32[2,512]{1,0:T(2,128)S(1)} %collective-permute-done.1, f32[2,512]{1,0:T(2,128)S(1)} %collective-permute-done, f32[2,512]{1,0:T(2,128)S(1)} %get-tuple-element.15), kind=kLoop, calls=%fused_computation.3 | loop fusion | flops 6144 | bytes 24576 | tf_op jit(solution)/shard_map/concatenate | solution.py:161
  41.7 0.0 all-to-all-done
  41.7 0.1 add_convert_fusion
  41.8 15.1 %all-gather = bf16[1,3072,128]{2,1,0:T(8,128)(2,1)S(1)} all-gather(bf16[1,768,128]{2,1,0:T(8,128)(2,1)S(1)} %add_convert_fusion), channel_id=2, replica_groups=mesh['cp'=128,'dp'=4] {'dp'}, dimensions={1}, use_global_device_ids=true | all-gather | bytes 983040 | tf_op jit(solution)/shard_map/all_gather | solution.py:166
  56.9 0.9 %slice_bitcast_fusion = (bf16[1536,128]{1,0:T(8,128)(2,1)}, bf16[1536,128]{1,0:T(8,128)(2,1)}) fusion(bf16[1,3072,128]{2,1,0:T(8,128)(2,1)S(1)} %all-gather), kind=kLoop, calls=%fused_computation | loop fusion | bytes 1572864 | tf_op jit(solution)/shard_map/slice | solution.py:167
  (1 shorter events, 0.0 us)
Async XLA Ops:
  0.6 0.7 %copy-start.1 = (s32[1,3]{1,0:T(1,128)S(1)}, s32[1,3]{1,0:T(1,128)}, u32[]{:S(2)}) copy-start(s32[1,3]{1,0:T(1,128)} %param.11) | copy-start | bytes 40
  11.5 4.5 %copy-start = (f32[3,2,512]{2,1,0:T(2,128)S(1)}, f32[3,2,512]{2,1,0:T(2,128)}, u32[]{:S(2)}) copy-start(f32[3,2,512]{2,1,0:T(2,128)} %get-tuple-element.12) | copy-start | bytes 36868
  11.5 30.2 %all-to-all-start = ((bf16[4,768,128]{2,1,0:T(8,128)(2,1)}), bf16[4,768,128]{2,1,0:T(8,128)(2,1)S(1)}, u32[]{:S(2)}, u32[]{:S(2)}) async-start(bf16[4,768,128]{2,1,0:T(8,128)(2,1)} %bitcast.12), calls=%async_computation | async-start | bytes 1572864 | tf_op jit(solution)/shard_map/all_to_all | solution.py:163
  16.0 20.0 %collective-permute-start.1 = (f32[2,512]{1,0:T(2,128)S(1)}, f32[2,512]{1,0:T(2,128)S(1)}, u32[]{:S(2)}, u32[]{:S(2)}) collective-permute-start(f32[2,512]{1,0:T(2,128)S(1)} %get-tuple-element.16), channel_id=1, source_target_pairs={{256,0},{260,4},{264,8},{268,12},{272,16},{276,20},{280,24},{284,2... | collective-permute-start | bytes 12296 | tf_op jit(solution)/shard_map/ppermute | solution.py:146
  31.7 9.4 %collective-permute-start = (f32[2,512]{1,0:T(2,128)S(1)}, f32[2,512]{1,0:T(2,128)S(1)}, u32[]{:S(2)}, u32[]{:S(2)}) collective-permute-start(f32[2,512]{1,0:T(2,128)S(1)} %get-tuple-element.17), channel_id=1, source_target_pairs={{384,0},{388,4},{392,8},{396,12},{400,16},{404,20},{408,24},{412,2... | collective-permute-start | bytes 12296 | tf_op jit(solution)/shard_map/ppermute | solution.py:146

commit v2 on v1

v2 whole, which is shorter than its diff:
```python
import functools
import math

import jax
import jax.numpy as jnp
from jax import lax
from jax.experimental import pallas as pl
from jax.experimental.pallas import tpu as pltpu
from jax.sharding import PartitionSpec as P


BLOCK = 128
NT = (((1,), (1,)), ((), ()))
NN = (((1,), (0,)), ((), ()))


def matmul(a, b, dims):
    return lax.dot_general(a, b, dims, preferred_element_type=jnp.float32)


def slot_of(hop, hop_table):
    slot = 0
    for s in range(1, hop_table.shape[1]):
        slot = slot + jnp.where(hop_table[0, s] == hop, s, 0)
    return slot


def row_at(block):
    return block * (block + 1) // 2 * BLOCK


def stacked(ref, block, heads, head_size):
    rows = slice(block * BLOCK, (block + 1) * BLOCK)
    return jnp.concatenate(
        [ref[rows, h * head_size : (h + 1) * head_size] for h in range(heads)], axis=0
    )


def key_side(
    hop_table,
    lengths,
    queries,
    keys,
    values,
    out_grad,
    partial,
    weights_out,
    score_grad_out,
    *rest,
    heads,
    scale,
):
    stats = rest[:-2]
    key_sum, value_sum = rest[-2:]
    rows, head_size = keys.shape
    blocks = rows // BLOCK
    wide = heads * BLOCK
    hop = pl.program_id(0)
    slot = slot_of(hop, hop_table)
    first_end = lengths[slot, 0]
    second_end = first_end + lengths[slot, 1]
    third_end = second_end + lengths[slot, 2]
    to_exp2 = scale * math.log2(math.e)
    lane = lax.broadcasted_iota(jnp.int32, (1, wide), 1) % BLOCK
    sublane = lax.broadcasted_iota(jnp.int32, (BLOCK, wide), 0)

    def products(block):
        span = (block + 1) * BLOCK
        query_rows = stacked(queries, block, heads, head_size)
        grad_rows = stacked(out_grad, block, heads, head_size)
        scores = matmul(keys[0:span, :], query_rows, NT)
        prob_grad = matmul(values[0:span, :], grad_rows, NT)
        return scores, prob_grad

    def soften(block, scores, prob_grad):
        begin = block * BLOCK
        row = lane + begin
        start = jnp.where(
            row >= third_end,
            third_end,
            jnp.where(row >= second_end, second_end, jnp.where(row >= first_end, first_end, 0)),
        )
        chunks = []
        peak = None
        for c in range(block + 1):
            allowed = sublane >= start - c * BLOCK
            if c == block:
                allowed = allowed & (sublane <= lane)
            chunk = jnp.where(allowed, scores[c * BLOCK : (c + 1) * BLOCK], -jnp.inf)
            chunks.append(chunk)
            peak = chunk if peak is None else jnp.maximum(peak, chunk)
        row_max = jnp.max(peak, axis=0, keepdims=True)
        total = None
        for c in range(block + 1):
            chunks[c] = jnp.exp2((chunks[c] - row_max) * to_exp2)
            total = chunks[c] if total is None else total + chunks[c]
        row_total = jnp.sum(total, axis=0, keepdims=True)
        share = 1.0 / row_total
        log_total = row_max * scale + jnp.log(row_total)
        for b in range(len(stats)):

            @pl.when(hop == b)
            def _(b=b):
                for h in range(heads):
                    stats[b][h : h + 1, begin : begin + BLOCK] = log_total[
                        :, h * BLOCK : (h + 1) * BLOCK
                    ]

        at = row_at(block)
        total = None
        for c in range(block + 1):
            chunks[c] = chunks[c] * share
            weights = chunks[c].astype(jnp.bfloat16)
            weights_out[0, at + c * BLOCK : at + (c + 1) * BLOCK, :] = weights
            part = weights.astype(jnp.float32) * prob_grad[c * BLOCK : (c + 1) * BLOCK]
            total = part if total is None else total + part
        delta = jnp.sum(total, axis=0, keepdims=True)
        for c in range(block + 1):
            score_grad = chunks[c] * (prob_grad[c * BLOCK : (c + 1) * BLOCK] - delta)
            score_grad_out[0, at + c * BLOCK : at + (c + 1) * BLOCK, :] = score_grad.astype(
                jnp.bfloat16
            )

    def gather_up(block):
        span = (block + 1) * BLOCK
        at = row_at(block)
        query_rows = stacked(queries, block, heads, head_size)
        grad_rows = stacked(out_grad, block, heads, head_size)
        value_part = matmul(weights_out[0, at : at + span, :], grad_rows, NN)
        key_part = matmul(score_grad_out[0, at : at + span, :], query_rows, NN)
        if block == blocks - 1:
            value_sum[...] = value_part
            key_sum[...] = key_part
        else:
            value_sum[0:span, :] += value_part
            key_sum[0:span, :] += key_part

    ready = products(blocks - 1)
    for block in reversed(range(blocks)):
        coming = products(block - 1) if block else None
        if block < blocks - 1:
            gather_up(block + 1)
        soften(block, *ready)
        ready = coming
    gather_up(0)
    partial[0] = (key_sum[...] * scale).astype(partial.dtype)
    partial[1] = value_sum[...].astype(partial.dtype)


def query_side(keys, values, weights, score_grad, attn_out, query_grad, *, heads, scale):
    rows, head_size = keys.shape
    value_cols = jnp.transpose(values[...])
    key_cols = jnp.transpose(keys[...])
    for block in range(rows // BLOCK):
        begin = block * BLOCK
        span = begin + BLOCK
        at = row_at(block)
        output = matmul(value_cols[:, 0:span], weights[0, at : at + span, :], NN)
        query_sum = matmul(key_cols[:, 0:span], score_grad[0, at : at + span, :], NN)
        output = jnp.transpose(output.astype(jnp.bfloat16))
        query_sum = jnp.transpose((query_sum * scale).astype(jnp.bfloat16))
        for h in range(heads):
            at = slice(h * BLOCK, (h + 1) * BLOCK)
            attn_out[begin:span, h * head_size : (h + 1) * head_size] = output[at]
            query_grad[begin:span, h * head_size : (h + 1) * head_size] = query_sum[at]


def key_side_call(hop_table, lengths, queries, keys, values, out_grad):
    slots = lengths.shape[0]
    rows = keys.shape[0] // slots
    head_size = keys.shape[1]
    width = queries.shape[1]
    heads = width // head_size
    wide = heads * BLOCK
    held = row_at(rows // BLOCK)
    at_slot = lambda i, hop_table, lengths: (slot_of(i, hop_table), 0)
    lifted = lambda i, hop_table, lengths: (slot_of(i, hop_table), 0, 0)
    wide_spec = pl.BlockSpec((rows, width), at_slot)
    narrow_spec = pl.BlockSpec((rows, head_size), at_slot)
    stats_spec = pl.BlockSpec((heads, rows), lambda i, hop_table, lengths: (0, 0))
    return pl.pallas_call(
        functools.partial(key_side, heads=heads, scale=head_size**-0.5),
        grid_spec=pltpu.PrefetchScalarGridSpec(
            num_scalar_prefetch=2,
            grid=(slots,),
            in_specs=[wide_spec, narrow_spec, narrow_spec, wide_spec],
            out_specs=[
                pl.BlockSpec(
                    (2, rows, head_size),
                    lambda i, hop_table, lengths: (0, slot_of(i, hop_table), 0),
                ),
                pl.BlockSpec((1, held, wide), lifted),
                pl.BlockSpec((1, held, wide), lifted),
            ]
            + [stats_spec] * slots,
            scratch_shapes=[
                pltpu.VMEM((rows, head_size), jnp.float32),
                pltpu.VMEM((rows, head_size), jnp.float32),
            ],
        ),
        out_shape=[
            jax.ShapeDtypeStruct((2,) + keys.shape, jnp.bfloat16),
            jax.ShapeDtypeStruct((slots, held, wide), jnp.bfloat16),
            jax.ShapeDtypeStruct((slots, held, wide), jnp.bfloat16),
        ]
        + [jax.ShapeDtypeStruct((heads, rows), jnp.float32)] * slots,
        name="key_side",
    )(hop_table, lengths, queries, keys, values, out_grad)


def query_side_call(keys, values, weights, score_grad, heads):
    slots, held, wide = weights.shape
    head_size = keys.shape[1]
    rows = keys.shape[0] // slots
    width = heads * head_size
    wide_spec = pl.BlockSpec((rows, width), lambda i: (i, 0))
    narrow_spec = pl.BlockSpec((rows, head_size), lambda i: (i, 0))
    held_spec = pl.BlockSpec((1, held, wide), lambda i: (i, 0, 0))
    return pl.pallas_call(
        functools.partial(query_side, heads=heads, scale=head_size**-0.5),
        grid=(slots,),
        in_specs=[narrow_spec, narrow_spec, held_spec, held_spec],
        out_specs=[wide_spec, wide_spec],
        out_shape=[jax.ShapeDtypeStruct((keys.shape[0], width), jnp.bfloat16)] * 2,
        name="query_side",
    )(keys, values, weights, score_grad)


def added(pieces, spread):
    total = pieces[0].astype(jnp.float32)
    for i in range(1, pieces.shape[0]):
        total = total + pieces[i].astype(jnp.float32)
    total = total.astype(spread.dtype)
    for i in range(spread.shape[0]):
        spread[i] = total


def added_call(pieces):
    return pl.pallas_call(
        added,
        in_specs=[pl.BlockSpec(memory_space=pltpu.VMEM)],
        out_specs=pl.BlockSpec(memory_space=pltpu.VMEM),
        out_shape=jax.ShapeDtypeStruct(pieces.shape, pieces.dtype),
        compiler_params=pltpu.CompilerParams(vmem_limit_bytes=16 << 20),
        name="added",
    )(pieces)


def passed_along(block, axis, distance):
    devices = range(lax.axis_size(axis))
    route = [((i - distance) % len(devices), i) for i in devices]
    return lax.ppermute(block, axis, route)


def local(queries, keys, values, out_grad, lengths, hop_table):
    heads = queries.shape[1] // keys.shape[1]
    cp_count = lax.axis_size("cp")
    dp_count = lax.axis_size("dp")
    partial, weights, score_grad, *stats = key_side_call(
        hop_table, lengths, queries, keys, values, out_grad
    )
    pieces = partial.reshape(dp_count, -1, partial.shape[-1])
    pieces = lax.all_to_all(pieces, "dp", 0, 0)
    near = passed_along(stats[1], "cp", cp_count >> 2)
    far = passed_along(stats[2], "cp", cp_count >> 1)
    spread = added_call(pieces)
    whole = lax.all_to_all(spread, "dp", 0, 0).reshape(partial.shape)
    attn_out, query_grad = query_side_call(keys, values, weights, score_grad, heads)
    row_stats = jnp.concatenate([stats[0], near, far], axis=1)
    return (attn_out, query_grad, whole[0], whole[1], row_stats)


def solution(mesh):
    return jax.shard_map(
        local,
        mesh=mesh,
        in_specs=(
            P("cp", "dp"),
            P("cp", None),
            P("cp", None),
            P("cp", "dp"),
            P("cp", None),
            P("cp", None),
        ),
        out_specs=(P("cp", "dp"), P("cp", "dp"), P("cp", None), P("cp", None), P("dp", "cp")),
        check_vma=False,
    )
```

time: 58.2 us -> 57.4 us (0.986)
  the two profiles are of different devices: /device:TPU:4 before, /device:TPU:8 now
where the time goes in v2:
time: 57.4 us; the launch traced here: 57 us
  starting transfers between devices  23.4 us (41%)
  blocking collectives  17.3 us (30%)
  Pallas kernels  14.1 us (25%)
  local copies, waits for them, and re-layouts  0.95 us (2%)
  between operations  0.68 us (1%)
  other arithmetic  0.61 us (1%)
    ppermute x2, starting transfers between devices, passed_along(): return lax.ppermute(block, axis, route)  18.5 us
    all_to_all x1, blocking collectives, local(): pieces = lax.all_to_all(pieces, 'dp', 0, 0)  17.3 us
    pallas_call x1, Pallas kernels, key_side_call(): pl.pallas_call(functools.partial(key_side, heads=heads, scale=head_size *...  8.17 us
    pallas_call x1, Pallas kernels, query_side_call(): pl.pallas_call(functools.partial(query_side, heads=heads, scale=head_size...  4.96 us
    all_to_all x1, starting transfers between devices, local(): whole = lax.all_to_all(spread, 'dp', 0, 0).reshape(partial.shape)  4.92 us
  transfers between devices with their start and end apart: 3, of which 0 were waited for; matrix products, arithmetic and copies ran while one was open for 1% of the time, Pallas kernels for 9%

profile of v2, /device:TPU:8, one launch (start us, length us, event | category | flops | bytes accessed | tf_op | source)
XLA Modules:
  0.0 57.0 jit_solution(4015547337374339994)
XLA Ops:
  0.6 8.2 %key_side.1 = (bf16[2,1536,128]{2,1,0:T(8,128)(2,1)}, bf16[3,1280,256]{2,1,0:T(8,128)(2,1)}, bf16[3,1280,256]{2,1,0:T(8,128)(2,1)}, f32[2,512]{1,0:T(2,128)}, f32[2,512]{1,0:T(2,128)}, /*index=5*/f32[2,512]{1,0:T(2,128)}) custom-call(s32[1,3]{1,0:T(1,128)} %hop_table.1, s32[3,4]{1,0:T(4,128)} %lengths.1, bf16[1536,256]{1,0:T(8,128)(2,1)} %queries.1, ...), custom_call_target="tpu_custom_call" | custom-call | tf_op jit(solution)/shard_map/key_side/pallas_call | solution.py:181
  8.8 17.3 %all_to_all.10.pieces = bf16[4,768,128]{2,1,0:T(8,128)(2,1)S(1)} all-to-all(bf16[4,768,128]{2,1,0:T(8,128)(2,1)} %bitcast.3), channel_id=1, replica_groups=mesh['cp'=128,'dp'=4] {'dp'}, dimensions={0} | all-to-all | bytes 1572864 | tf_op jit(solution)/shard_map/all_to_all | solution.py:263
  26.1 0.0 copy-start.2
  26.1 0.0 copy-start.1
  26.1 1.0 %added.1 = bf16[4,768,128]{2,1,0:T(8,128)(2,1)} custom-call(bf16[4,768,128]{2,1,0:T(8,128)(2,1)S(1)} %all_to_all.10.pieces), custom_call_target="tpu_custom_call" | custom-call | tf_op jit(solution)/shard_map/added/pallas_call | solution.py:239
  27.1 4.9 %all-to-all-start.1 = ((bf16[4,768,128]{2,1,0:T(8,128)(2,1)}), bf16[4,768,128]{2,1,0:T(8,128)(2,1)S(1)}, u32[]{:S(2)}, u32[]{:S(2)}) async-start(bf16[4,768,128]{2,1,0:T(8,128)(2,1)} %added.1), calls=%async_computation.1 | async-start | bytes 1572864 | tf_op jit(solution)/shard_map/all_to_all | solution.py:267
  32.0 0.0 copy-done.2
  32.0 7.5 %collective-permute-start = (f32[2,512]{1,0:T(2,128)S(1)}, f32[2,512]{1,0:T(2,128)S(1)}, u32[]{:S(2)}, u32[]{:S(2)}) collective-permute-start(f32[2,512]{1,0:T(2,128)S(1)} %copy-done.2), channel_id=1, source_target_pairs={{384,0},{388,4},{392,8},{396,12},{400,16},{404,20},{408,24},{412,2... | collective-permute-start | bytes 12296 | tf_op jit(solution)/shard_map/ppermute | solution.py:252
  39.5 0.0 copy-done.1
  39.6 10.9 %collective-permute-start.1 = (f32[2,512]{1,0:T(2,128)S(1)}, f32[2,512]{1,0:T(2,128)S(1)}, u32[]{:S(2)}, u32[]{:S(2)}) collective-permute-start(f32[2,512]{1,0:T(2,128)S(1)} %copy-done.1), channel_id=1, source_target_pairs={{256,0},{260,4},{264,8},{268,12},{272,16},{276,20},{280,24},{284,2... | collective-permute-start | bytes 12296 | tf_op jit(solution)/shard_map/ppermute | solution.py:252
  50.5 0.0 copy-start
  50.5 5.0 %query_side.1 = (bf16[1536,256]{1,0:T(8,128)(2,1)}, bf16[1536,256]{1,0:T(8,128)(2,1)}) custom-call(bf16[1536,128]{1,0:T(8,128)(2,1)} %keys.3, bf16[1536,128]{1,0:T(8,128)(2,1)} %values.3, bf16[3,1280,256]{2,1,0:T(8,128)(2,1)} %get-tuple-element.13.weights, bf16[3,1280,256]{2,1,0:T(8,128)(2,1)} %get-tuple-element.14.score_grad), custom_call_target="tpu_custom_call" | custom-call | tf_op jit(solution)/shard_map/query_side/pallas_call | solution.py:219
  55.5 0.0 collective-permute-done
  55.5 0.0 collective-permute-done.1
  55.5 0.0 copy-done
  55.5 0.6 %pad_maximum_fusion = f32[2,1536]{1,0:T(2,128)} fusion(f32[2,512]{1,0:T(2,128)S(1)} %collective-permute-done.1, f32[2,512]{1,0:T(2,128)S(1)} %collective-permute-done, f32[2,512]{1,0:T(2,128)S(1)} %copy-done), kind=kLoop, calls=%fused_computation | loop fusion | flops 6144 | bytes 24576 | tf_op jit(solution)/shard_map/concatenate | solution.py:269
  56.1 0.0 all-to-all-done.1
  56.1 0.9 %fusion = (bf16[2,768,128]{2,1,0:T(8,128)(2,1)}, bf16[2,768,128]{2,1,0:T(8,128)(2,1)}) fusion(bf16[4,768,128]{2,1,0:T(8,128)(2,1)S(1)} %all-to-all-done.1), kind=kLoop, calls=%fused_computation.1 | loop fusion | bytes 1572864 | tf_op jit(solution)/shard_map/slice | solution.py:270
Async XLA Ops:
  26.1 5.9 %copy-start.2 = (f32[2,512]{1,0:T(2,128)S(1)}, f32[2,512]{1,0:T(2,128)}, u32[]{:S(2)}) copy-start(f32[2,512]{1,0:T(2,128)} %get-tuple-element.19) | copy-start | bytes 12292
  26.1 13.5 %copy-start.1 = (f32[2,512]{1,0:T(2,128)S(1)}, f32[2,512]{1,0:T(2,128)}, u32[]{:S(2)}) copy-start(f32[2,512]{1,0:T(2,128)} %get-tuple-element.20) | copy-start | bytes 12292
  27.1 29.0 %all-to-all-start.1 = ((bf16[4,768,128]{2,1,0:T(8,128)(2,1)}), bf16[4,768,128]{2,1,0:T(8,128)(2,1)S(1)}, u32[]{:S(2)}, u32[]{:S(2)}) async-start(bf16[4,768,128]{2,1,0:T(8,128)(2,1)} %added.1), calls=%async_computation.1 | async-start | bytes 1572864 | tf_op jit(solution)/shard_map/all_to_all | solution.py:267
  32.0 23.5 %collective-permute-start = (f32[2,512]{1,0:T(2,128)S(1)}, f32[2,512]{1,0:T(2,128)S(1)}, u32[]{:S(2)}, u32[]{:S(2)}) collective-permute-start(f32[2,512]{1,0:T(2,128)S(1)} %copy-done.2), channel_id=1, source_target_pairs={{384,0},{388,4},{392,8},{396,12},{400,16},{404,20},{408,24},{412,2... | collective-permute-start | bytes 12296 | tf_op jit(solution)/shard_map/ppermute | solution.py:252
  39.6 15.9 %collective-permute-start.1 = (f32[2,512]{1,0:T(2,128)S(1)}, f32[2,512]{1,0:T(2,128)S(1)}, u32[]{:S(2)}, u32[]{:S(2)}) collective-permute-start(f32[2,512]{1,0:T(2,128)S(1)} %copy-done.1), channel_id=1, source_target_pairs={{256,0},{260,4},{264,8},{268,12},{272,16},{276,20},{280,24},{284,2... | collective-permute-start | bytes 12296 | tf_op jit(solution)/shard_map/ppermute | solution.py:252
  50.5 5.0 %copy-start = (f32[2,512]{1,0:T(2,128)S(1)}, f32[2,512]{1,0:T(2,128)}, u32[]{:S(2)}) copy-start(f32[2,512]{1,0:T(2,128)} %get-tuple-element.18) | copy-start | bytes 12292

commit v3 on v2

--- a/solution.py
+++ b/solution.py
@@ -50,8 +50,7 @@
     heads,
     scale,
 ):
-    stats = rest[:-2]
-    key_sum, value_sum = rest[-2:]
+    kept_stats, moved_stats, key_sum, value_sum, stats = rest
     rows, head_size = keys.shape
     blocks = rows // BLOCK
     wide = heads * BLOCK
@@ -97,14 +96,10 @@
         row_total = jnp.sum(total, axis=0, keepdims=True)
         share = 1.0 / row_total
         log_total = row_max * scale + jnp.log(row_total)
-        for b in range(len(stats)):
-
-            @pl.when(hop == b)
-            def _(b=b):
-                for h in range(heads):
-                    stats[b][h : h + 1, begin : begin + BLOCK] = log_total[
-                        :, h * BLOCK : (h + 1) * BLOCK
-                    ]
+        for h in range(heads):
+            stats[pl.ds(hop, 1), h : h + 1, begin : begin + BLOCK] = log_total[
+                None, :, h * BLOCK : (h + 1) * BLOCK
+            ]
 
         at = row_at(block)
         total = None
@@ -145,6 +140,11 @@
     gather_up(0)
     partial[0] = (key_sum[...] * scale).astype(partial.dtype)
     partial[1] = value_sum[...].astype(partial.dtype)
+
+    @pl.when(hop == pl.num_programs(0) - 1)
+    def _():
+        kept_stats[...] = stats[0]
+        moved_stats[...] = stats[1:]
 
 
 def query_side(keys, values, weights, score_grad, attn_out, query_grad, *, heads, scale):
@@ -177,7 +177,6 @@
     lifted = lambda i, hop_table, lengths: (slot_of(i, hop_table), 0, 0)
     wide_spec = pl.BlockSpec((rows, width), at_slot)
     narrow_spec = pl.BlockSpec((rows, head_size), at_slot)
-    stats_spec = pl.BlockSpec((heads, rows), lambda i, hop_table, lengths: (0, 0))
     return pl.pallas_call(
         functools.partial(key_side, heads=heads, scale=head_size**-0.5),
         grid_spec=pltpu.PrefetchScalarGridSpec(
@@ -192,10 +191,14 @@
                 pl.BlockSpec((1, held, wide), lifted),
                 pl.BlockSpec((1, held, wide), lifted),
             ]
-            + [stats_spec] * slots,
+            + [
+                pl.BlockSpec((heads, rows), lambda i, hop_table, lengths: (0, 0)),
+                pl.BlockSpec((slots - 1, heads, rows), lambda i, hop_table, lengths: (0, 0, 0)),
+            ],
             scratch_shapes=[
                 pltpu.VMEM((rows, head_size), jnp.float32),
                 pltpu.VMEM((rows, head_size), jnp.float32),
+                pltpu.VMEM((slots, heads, rows), jnp.float32),
             ],
         ),
         out_shape=[
@@ -203,7 +206,10 @@
             jax.ShapeDtypeStruct((slots, held, wide), jnp.bfloat16),
             jax.ShapeDtypeStruct((slots, held, wide), jnp.bfloat16),
         ]
-        + [jax.ShapeDtypeStruct((heads, rows), jnp.float32)] * slots,
+        + [
+            jax.ShapeDtypeStruct((heads, rows), jnp.float32),
+            jax.ShapeDtypeStruct((slots - 1, heads, rows), jnp.float32),
+        ],
         name="key_side",
     )(hop_table, lengths, queries, keys, values, out_grad)
 
@@ -256,17 +262,17 @@
     heads = queries.shape[1] // keys.shape[1]
     cp_count = lax.axis_size("cp")
     dp_count = lax.axis_size("dp")
-    partial, weights, score_grad, *stats = key_side_call(
+    partial, weights, score_grad, kept_stats, moved_stats = key_side_call(
         hop_table, lengths, queries, keys, values, out_grad
     )
     pieces = partial.reshape(dp_count, -1, partial.shape[-1])
     pieces = lax.all_to_all(pieces, "dp", 0, 0)
-    near = passed_along(stats[1], "cp", cp_count >> 2)
-    far = passed_along(stats[2], "cp", cp_count >> 1)
+    near = passed_along(moved_stats, "cp", cp_count >> 2)
+    far = passed_along(near, "cp", cp_count >> 2)
     spread = added_call(pieces)
     whole = lax.all_to_all(spread, "dp", 0, 0).reshape(partial.shape)
     attn_out, query_grad = query_side_call(keys, values, weights, score_grad, heads)
-    row_stats = jnp.concatenate([stats[0], near, far], axis=1)
+    row_stats = jnp.concatenate([kept_stats, near[0], far[1]], axis=1)
     return (attn_out, query_grad, whole[0], whole[1], row_stats)
 
 

time: 57.4 us -> 54.1 us (0.943)
  the two profiles are of different devices: /device:TPU:8 before, /device:TPU:4 now
where the time goes in v3:
time: 54.1 us; the launch traced here: 53.7 us
  starting transfers between devices  26.9 us (50%)
  Pallas kernels  13.5 us (25%)
  waiting for transfers between devices  11.1 us (21%)
  local copies, waits for them, and re-layouts  0.94 us (2%)
  between operations  0.67 us (1%)
  other arithmetic  0.61 us (1%)
    ppermute x2, starting transfers between devices, passed_along(): return lax.ppermute(block, axis, route)  17.7 us
    all_to_all x1, waiting for transfers between devices, local(): whole = lax.all_to_all(spread, 'dp', 0, 0).reshape(partial.shape)  10.5 us
    pallas_call x1, Pallas kernels, key_side_call(): pl.pallas_call(functools.partial(key_side, heads=heads, scale=head_size *...  7.53 us
    pallas_call x1, Pallas kernels, query_side_call(): pl.pallas_call(functools.partial(query_side, heads=heads, scale=head_size...  4.96 us
    all_to_all x1, starting transfers between devices, local(): whole = lax.all_to_all(spread, 'dp', 0, 0).reshape(partial.shape)  4.79 us
    all_to_all x1, starting transfers between devices, local(): pieces = lax.all_to_all(pieces, 'dp', 0, 0)  4.46 us
  transfers between devices with their start and end apart: 4, of which 2 were waited for; matrix products, arithmetic and copies ran while one was open for 1% of the time, Pallas kernels for 11%

profile of v3, /device:TPU:4, one launch (start us, length us, event | category | flops | bytes accessed | tf_op | source)
XLA Modules:
  0.0 53.7 jit_solution(4444152176247448402)
XLA Ops:
  0.6 7.5 %key_side.1 = (bf16[2,1536,128]{2,1,0:T(8,128)(2,1)}, bf16[3,1280,256]{2,1,0:T(8,128)(2,1)}, bf16[3,1280,256]{2,1,0:T(8,128)(2,1)}, f32[2,512]{1,0:T(2,128)}, f32[2,2,512]{2,1,0:T(2,128)}) custom-call(s32[1,3]{1,0:T(1,128)} %hop_table.1, s32[3,4]{1,0:T(4,128)} %lengths.1, bf16[1536,256]{1,0:T(8,128)(2,1)} %queries.1, bf16[1536,128]{1,0:T(8,128)(2,1)} %keys.3, ...), custom_call_target="tpu_custom_call" | custom-call | tf_op jit(solution)/shard_map/key_side/pallas_call | solution.py:180
  8.2 4.5 %all-to-all-start = ((bf16[4,768,128]{2,1,0:T(8,128)(2,1)}), bf16[4,768,128]{2,1,0:T(8,128)(2,1)S(1)}, u32[]{:S(2)}, u32[]{:S(2)}) async-start(bf16[4,768,128]{2,1,0:T(8,128)(2,1)} %bitcast.7), calls=%async_computation | async-start | bytes 1572864 | tf_op jit(solution)/shard_map/all_to_all | solution.py:269
  12.6 9.1 %collective-permute-start = (f32[2,2,512]{2,1,0:T(2,128)}, f32[2,2,512]{2,1,0:T(2,128)S(1)}, u32[]{:S(2)}, u32[]{:S(2)}) collective-permute-start(f32[2,2,512]{2,1,0:T(2,128)} %get-tuple-element.18), channel_id=1, source_target_pairs={{384,0},{388,4},{392,8},{396,12},{400,16},{404,20},{408,24},{412,2... | collective-permute-start | bytes 24584 | tf_op jit(solution)/shard_map/ppermute | solution.py:258
  21.7 5.0 %query_side.1 = (bf16[1536,256]{1,0:T(8,128)(2,1)}, bf16[1536,256]{1,0:T(8,128)(2,1)}) custom-call(bf16[1536,128]{1,0:T(8,128)(2,1)} %keys.3, bf16[1536,128]{1,0:T(8,128)(2,1)} %values.3, bf16[3,1280,256]{2,1,0:T(8,128)(2,1)} %get-tuple-element.12.weights, bf16[3,1280,256]{2,1,0:T(8,128)(2,1)} %get-tuple-element.13.score_grad), custom_call_target="tpu_custom_call" | custom-call | tf_op jit(solution)/shard_map/query_side/pallas_call | solution.py:225
  26.7 0.0 copy-start
  26.7 0.5 collective-permute-done
  27.2 8.6 %collective-permute-start.1 = (f32[2,2,512]{2,1,0:T(2,128)S(1)}, f32[2,2,512]{2,1,0:T(2,128)S(1)}, u32[]{:S(2)}, u32[]{:S(2)}) collective-permute-start(f32[2,2,512]{2,1,0:T(2,128)S(1)} %collective-permute-done), channel_id=1, source_target_pairs={{384,0},{388,4},{392,8},{396,12},{400,16},{404,20},{408,24},{412,2... | collective-permute-start | bytes 24584 | tf_op jit(solution)/shard_map/ppermute | solution.py:258
  35.8 0.0 all-to-all-done.pieces
  35.8 1.0 %added.1 = bf16[4,768,128]{2,1,0:T(8,128)(2,1)} custom-call(bf16[4,768,128]{2,1,0:T(8,128)(2,1)S(1)} %all-to-all-done.pieces), custom_call_target="tpu_custom_call" | custom-call | tf_op jit(solution)/shard_map/added/pallas_call | solution.py:245
  36.8 4.8 %all-to-all-start.1 = ((bf16[4,768,128]{2,1,0:T(8,128)(2,1)}), bf16[4,768,128]{2,1,0:T(8,128)(2,1)S(1)}, u32[]{:S(2)}, u32[]{:S(2)}) async-start(bf16[4,768,128]{2,1,0:T(8,128)(2,1)} %added.1), calls=%async_computation.1 | async-start | bytes 1572864 | tf_op jit(solution)/shard_map/all_to_all | solution.py:273
  41.6 0.0 collective-permute-done.1
  41.6 0.0 copy-done
  41.6 0.6 %pad_maximum_fusion = f32[2,1536]{1,0:T(2,128)} fusion(f32[2,512]{1,0:T(2,128)S(1)} %slice_bitcast_fusion, f32[2,512]{1,0:T(2,128)S(1)} %slice_bitcast_fusion.1, f32[2,512]{1,0:T(2,128)S(1)} %copy-done), kind=kLoop, calls=%fused_computation | loop fusion | flops 6144 | bytes 24576 | tf_op jit(solution)/shard_map/concatenate | solution.py:275
  42.2 10.5 %all-to-all-done.1 = bf16[4,768,128]{2,1,0:T(8,128)(2,1)S(1)} async-done(((bf16[4,768,128]{2,1,0:T(8,128)(2,1)}), bf16[4,768,128]{2,1,0:T(8,128)(2,1)S(1)}, u32[]{:S(2)}, u32[]{:S(2)}) %all-to-all-start.1) | async-done | bytes 786464 | tf_op jit(solution)/shard_map/all_to_all | solution.py:273
  52.8 0.9 %fusion = (bf16[2,768,128]{2,1,0:T(8,128)(2,1)}, bf16[2,768,128]{2,1,0:T(8,128)(2,1)}) fusion(bf16[4,768,128]{2,1,0:T(8,128)(2,1)S(1)} %all-to-all-done.1), kind=kLoop, calls=%fused_computation.3 | loop fusion | bytes 1572864 | tf_op jit(solution)/shard_map/slice | solution.py:276
  (2 shorter events, 0.0 us)
Async XLA Ops:
  8.2 27.6 %all-to-all-start = ((bf16[4,768,128]{2,1,0:T(8,128)(2,1)}), bf16[4,768,128]{2,1,0:T(8,128)(2,1)S(1)}, u32[]{:S(2)}, u32[]{:S(2)}) async-start(bf16[4,768,128]{2,1,0:T(8,128)(2,1)} %bitcast.7), calls=%async_computation | async-start | bytes 1572864 | tf_op jit(solution)/shard_map/all_to_all | solution.py:269
  12.6 14.6 %collective-permute-start = (f32[2,2,512]{2,1,0:T(2,128)}, f32[2,2,512]{2,1,0:T(2,128)S(1)}, u32[]{:S(2)}, u32[]{:S(2)}) collective-permute-start(f32[2,2,512]{2,1,0:T(2,128)} %get-tuple-element.18), channel_id=1, source_target_pairs={{384,0},{388,4},{392,8},{396,12},{400,16},{404,20},{408,24},{412,2... | collective-permute-start | bytes 24584 | tf_op jit(solution)/shard_map/ppermute | solution.py:258
  26.7 14.9 %copy-start = (f32[2,512]{1,0:T(2,128)S(1)}, f32[2,512]{1,0:T(2,128)}, u32[]{:S(2)}) copy-start(f32[2,512]{1,0:T(2,128)} %get-tuple-element.17) | copy-start | bytes 12292
  27.2 14.4 %collective-permute-start.1 = (f32[2,2,512]{2,1,0:T(2,128)S(1)}, f32[2,2,512]{2,1,0:T(2,128)S(1)}, u32[]{:S(2)}, u32[]{:S(2)}) collective-permute-start(f32[2,2,512]{2,1,0:T(2,128)S(1)} %collective-permute-done), channel_id=1, source_target_pairs={{384,0},{388,4},{392,8},{396,12},{400,16},{404,20},{408,24},{412,2... | collective-permute-start | bytes 24584 | tf_op jit(solution)/shard_map/ppermute | solution.py:258
  36.8 16.0 %all-to-all-start.1 = ((bf16[4,768,128]{2,1,0:T(8,128)(2,1)}), bf16[4,768,128]{2,1,0:T(8,128)(2,1)S(1)}, u32[]{:S(2)}, u32[]{:S(2)}) async-start(bf16[4,768,128]{2,1,0:T(8,128)(2,1)} %added.1), calls=%async_computation.1 | async-start | bytes 1572864 | tf_op jit(solution)/shard_map/all_to_all | solution.py:273
